TPU v7x, 64 devices: a 2x2x8 block of a 4x4x8 slice. The times are simulated.
64 devices in a mesh: dp: 4 (over x, y), ep: 16 (over z, core).
Axes of the slice: x: 2, y: 2, z: 8, core: 2. Of those that a mesh axis runs over, the one named last changes fastest.
The devices are a block of a 4x4x8 slice.
Arguments:
- tokens: bfloat16 [65536, 1024], P(('dp', 'ep')), parts along dimension 0
- route_idx: int32 [65536, 8], P(('dp', 'ep')), parts along dimension 0
- gate_vals: float32 [65536, 8], P(('dp', 'ep')), parts along dimension 0
- w_gate: bfloat16 [32, 1024, 512], P('ep')
- w_up: bfloat16 [32, 1024, 512], P('ep')
- w_down: bfloat16 [32, 512, 1024], P('ep')
Outputs:
- output: bfloat16 [65536, 1024], P(('dp', 'ep')), parts along dimension 0
There are 4 independent parts. A program takes and returns all parts, laid end to end along the dimension named above; an argument that names none is the same for every part.
All inputs are finite; a program needn't handle non-finite values.
Results may differ from a plain program's by a relative error of at most 0.00782001.
Values are sent between devices in bfloat16 or wider.
A program may use at most 768 MiB of HBM per device.

v0:
```python
import jax
import jax.numpy as jnp
from jax import lax
from jax.sharding import PartitionSpec as P


def pack_index(route_loc, n_experts, capacity):
    hit_mask = route_loc[:, :, None] == jnp.arange(n_experts)
    member = jnp.sum(hit_mask, axis=1, dtype=jnp.int32)
    running = jnp.cumsum(member, axis=0)
    targets = jnp.arange(capacity) + 1
    row_ids = jax.vmap(lambda column: jnp.searchsorted(column, targets, side="left"), in_axes=1)(running)
    slot_pos = jnp.take_along_axis(running, route_loc, axis=1) - 1
    return row_ids, slot_pos


def combine_rows(returned, flat_pos, gate_loc):
    picked = jnp.take(returned, flat_pos, axis=0)
    return jnp.sum(gate_loc[:, :, None] * picked.astype(jnp.float32), axis=1).astype(jnp.bfloat16)


def expert_ffn(rows_in, wg_loc, wu_loc, wd_loc):
    pre_gate = jnp.einsum("erd,edf->erf", rows_in, wg_loc, preferred_element_type=jnp.float32)
    pre_up = jnp.einsum("erd,edf->erf", rows_in, wu_loc, preferred_element_type=jnp.float32)
    hidden = (jax.nn.silu(pre_gate) * pre_up).astype(jnp.bfloat16)
    return jnp.einsum("erf,efd->erd", hidden, wd_loc, preferred_element_type=jnp.float32).astype(jnp.bfloat16)


def solution(mesh):
    group_n = mesh.shape["ep"]
    row_spec = P(("dp", "ep"))
    expert_spec = P("ep")

    def local_step(tok_loc, route_loc, gate_loc, wg_loc, wu_loc, wd_loc):
        local_n = wg_loc.shape[0]
        tok_dev, d_model = tok_loc.shape
        capacity = tok_dev // 2
        row_ids, slot_pos = pack_index(route_loc, local_n * group_n, capacity)
        row_ids = row_ids.reshape(group_n, local_n, capacity).transpose(1, 0, 2)
        send_buf = jnp.take(tok_loc, row_ids, axis=0, mode="fill", fill_value=0)
        recv_buf = lax.all_to_all(send_buf, "ep", 1, 1, tiled=True)
        expert_out = expert_ffn(recv_buf.reshape(local_n, group_n * capacity, d_model), wg_loc, wu_loc, wd_loc)
        returned = lax.all_to_all(expert_out.reshape(local_n, group_n, capacity, d_model), "ep", 1, 1, tiled=True)
        flat_pos = ((route_loc % local_n) * group_n + route_loc // local_n) * capacity + slot_pos
        return combine_rows(returned.reshape(-1, d_model), flat_pos, gate_loc)

    return jax.shard_map(local_step, mesh=mesh, in_specs=(row_spec, row_spec, row_spec, expert_spec, expert_spec, expert_spec), out_specs=row_spec, check_vma=False)
```

profile of v0, /device:TPU:21, one launch (start us, length us, event | category | flops | bytes accessed | tf_op | source)
XLA Modules:
  0.0 3343.9 jit_solution(15171040288891338770)
XLA Ops:
  0.0 1.0 convert_reduce_fusion
  1.1 9.0 reduce-window.6
  10.1 0.1 slice.16
  10.2 0.1 copy.57
  10.3 0.1 copy.58
  10.4 0.1 broadcast_add_fusion
  10.6 1426.6 %while.24 = (s32[]{:T(128)}, u32[32,512]{1,0:T(8,128)S(1)}, u32[32,512]{1,0:T(8,128)S(1)}, s32[32,1024]{1,0:T(8,128)S(1)}, s32[]{:T(128)}, /*index=5*/s32[]{:T(128)}) while((s32[]{:T(128)}, u32[32,512]{1,0:T(8,128)S(1)}, u32[32,512]{1,0:T(8,128)S(1)}, s32[32,1024]{1,0:T(8,128)S(1)}, s32[]{:T(128)}, /*index=5*/s32[]{:T(128)}) %tuple.39), condition=%wide.region_4.5_spmd.clone, body=%wide.region_3.4_spmd.clone.sunk | while | flops 377347 | bytes 1347665 | solution.py:12
  10.6 129.5 %gather_fusion = s32[16384]{0:T(1024)S(1)} fusion(s32[32,1024]{1,0:T(8,128)S(1)} %get-tuple-element.146, u32[16384]{0:T(1024)S(1)} %bitcast.57), kind=kCustom, calls=%fused_computation.clone.clone.1 | custom fusion | bytes 262144 | tf_op jit(solution)/shard_map/vmap(jit(searchsorted))/vmap(jit(_searchsorted_scan_impl))/while/body/eval_jaxpr/gather | solution.py:12
  140.2 0.1 select_select_fusion.5
  140.3 129.5 %gather_fusion = s32[16384]{0:T(1024)S(1)} fusion(s32[32,1024]{1,0:T(8,128)S(1)} %get-tuple-element.146, u32[16384]{0:T(1024)S(1)} %bitcast.57), kind=kCustom, calls=%fused_computation.clone.clone.1 | custom fusion | bytes 262144 | tf_op jit(solution)/shard_map/vmap(jit(searchsorted))/vmap(jit(_searchsorted_scan_impl))/while/body/eval_jaxpr/gather | solution.py:12
  269.9 0.1 select_select_fusion.5
  270.0 129.5 %gather_fusion = s32[16384]{0:T(1024)S(1)} fusion(s32[32,1024]{1,0:T(8,128)S(1)} %get-tuple-element.146, u32[16384]{0:T(1024)S(1)} %bitcast.57), kind=kCustom, calls=%fused_computation.clone.clone.1 | custom fusion | bytes 262144 | tf_op jit(solution)/shard_map/vmap(jit(searchsorted))/vmap(jit(_searchsorted_scan_impl))/while/body/eval_jaxpr/gather | solution.py:12
  399.6 0.1 select_select_fusion.5
  399.7 129.5 %gather_fusion = s32[16384]{0:T(1024)S(1)} fusion(s32[32,1024]{1,0:T(8,128)S(1)} %get-tuple-element.146, u32[16384]{0:T(1024)S(1)} %bitcast.57), kind=kCustom, calls=%fused_computation.clone.clone.1 | custom fusion | bytes 262144 | tf_op jit(solution)/shard_map/vmap(jit(searchsorted))/vmap(jit(_searchsorted_scan_impl))/while/body/eval_jaxpr/gather | solution.py:12
  529.3 0.1 select_select_fusion.5
  529.4 129.5 %gather_fusion = s32[16384]{0:T(1024)S(1)} fusion(s32[32,1024]{1,0:T(8,128)S(1)} %get-tuple-element.146, u32[16384]{0:T(1024)S(1)} %bitcast.57), kind=kCustom, calls=%fused_computation.clone.clone.1 | custom fusion | bytes 262144 | tf_op jit(solution)/shard_map/vmap(jit(searchsorted))/vmap(jit(_searchsorted_scan_impl))/while/body/eval_jaxpr/gather | solution.py:12
  659.1 129.5 %gather_fusion = s32[16384]{0:T(1024)S(1)} fusion(s32[32,1024]{1,0:T(8,128)S(1)} %get-tuple-element.146, u32[16384]{0:T(1024)S(1)} %bitcast.57), kind=kCustom, calls=%fused_computation.clone.clone.1 | custom fusion | bytes 262144 | tf_op jit(solution)/shard_map/vmap(jit(searchsorted))/vmap(jit(_searchsorted_scan_impl))/while/body/eval_jaxpr/gather | solution.py:12
  788.8 129.5 %gather_fusion = s32[16384]{0:T(1024)S(1)} fusion(s32[32,1024]{1,0:T(8,128)S(1)} %get-tuple-element.146, u32[16384]{0:T(1024)S(1)} %bitcast.57), kind=kCustom, calls=%fused_computation.clone.clone.1 | custom fusion | bytes 262144 | tf_op jit(solution)/shard_map/vmap(jit(searchsorted))/vmap(jit(_searchsorted_scan_impl))/while/body/eval_jaxpr/gather | solution.py:12
  918.3 0.1 select_select_fusion.5
  918.5 129.5 %gather_fusion = s32[16384]{0:T(1024)S(1)} fusion(s32[32,1024]{1,0:T(8,128)S(1)} %get-tuple-element.146, u32[16384]{0:T(1024)S(1)} %bitcast.57), kind=kCustom, calls=%fused_computation.clone.clone.1 | custom fusion | bytes 262144 | tf_op jit(solution)/shard_map/vmap(jit(searchsorted))/vmap(jit(_searchsorted_scan_impl))/while/body/eval_jaxpr/gather | solution.py:12
  1048.0 0.1 select_select_fusion.5
  1048.2 129.5 %gather_fusion = s32[16384]{0:T(1024)S(1)} fusion(s32[32,1024]{1,0:T(8,128)S(1)} %get-tuple-element.146, u32[16384]{0:T(1024)S(1)} %bitcast.57), kind=kCustom, calls=%fused_computation.clone.clone.1 | custom fusion | bytes 262144 | tf_op jit(solution)/shard_map/vmap(jit(searchsorted))/vmap(jit(_searchsorted_scan_impl))/while/body/eval_jaxpr/gather | solution.py:12
  1177.9 129.5 %gather_fusion = s32[16384]{0:T(1024)S(1)} fusion(s32[32,1024]{1,0:T(8,128)S(1)} %get-tuple-element.146, u32[16384]{0:T(1024)S(1)} %bitcast.57), kind=kCustom, calls=%fused_computation.clone.clone.1 | custom fusion | bytes 262144 | tf_op jit(solution)/shard_map/vmap(jit(searchsorted))/vmap(jit(_searchsorted_scan_impl))/while/body/eval_jaxpr/gather | solution.py:12
  1307.6 129.5 %gather_fusion = s32[16384]{0:T(1024)S(1)} fusion(s32[32,1024]{1,0:T(8,128)S(1)} %get-tuple-element.146, u32[16384]{0:T(1024)S(1)} %bitcast.57), kind=kCustom, calls=%fused_computation.clone.clone.1 | custom fusion | bytes 262144 | tf_op jit(solution)/shard_map/vmap(jit(searchsorted))/vmap(jit(_searchsorted_scan_impl))/while/body/eval_jaxpr/gather | solution.py:12
  1437.1 0.1 select_select_fusion.5
  1437.4 69.7 %gather_fusion.1 = bf16[16384,1024]{1,0:T(8,128)(2,1)} fusion(bf16[1024,1024]{1,0:T(8,128)(2,1)S(1)} %copy-done, s32[16384]{0:T(1024)S(1)} %broadcast_clamp_fusion), kind=kCustom, calls=%fused_computation.1 | custom fusion | bytes 67174400 | tf_op jit(solution)/shard_map/jit(_take)/gather | solution.py:40
  1507.2 22.8 copy_select_fusion
  1530.0 733.4 %all_to_all.10 = bf16[2,16,512,1024]{3,2,0,1:T(8,128)(2,1)} all-to-all(bf16[2,16,512,1024]{3,2,0,1:T(8,128)(2,1)} %copy_select_fusion), channel_id=1, replica_groups=mesh['dp'=4,'ep'=16] {'ep'}, dimensions={1} | all-to-all | bytes 67108864 | tf_op jit(solution)/shard_map/all_to_all | solution.py:41
  2263.4 22.8 copy.65
  2286.2 31.7 fusion.16
  2317.9 47.6 %convolution_convert_fusion = bf16[2,8192,1024]{2,1,0:T(8,128)(2,1)} fusion(bf16[2,512,1024]{2,1,0:T(8,128)(2,1)} %param.13, f32[2,8192,512]{2,1,0:T(8,128)} %fusion.16, bf16[2,8192,1024]{2,1,0:T(8,128)(2,1)} %bitcast.61, bf16[2,1024,512]{2,1,0:T(8,128)(2,1)} %param.12), kind=kOutput, calls=%fused_computation.15 | convolution fusion | flops 34426847232 | bytes 104857600 | tf_op jit(solution)/shard_map/erf,efd->erd/dot_general | solution.py:26
  2365.5 22.7 copy.66
  2388.2 6.4 all-to-all-start.1
  2394.6 0.2 copy.59
  2394.8 0.3 reshape.74
  2395.1 0.4 copy-done.3
  2395.5 65.5 %gather_fusion.3 = s32[8192]{0:T(1024)S(1)} fusion(s32[1024,32]{0,1:T(8,128)S(1)} %bitcast.56, s32[8192]{0:T(1024)S(1)} %reshape.74), kind=kCustom, calls=%fused_computation.3 | custom fusion | bytes 131072 | tf_op jit(solution)/shard_map/jit(take_along_axis)/gather | solution.py:13
  2461.0 0.3 reshape.77
  2461.3 0.2 copy.60
  2461.5 0.1 compare_and_fusion.1
  2461.6 0.2 copy.68
  2461.8 0.3 reshape.68
  2462.0 0.3 copy.61
  2462.3 0.2 copy.56
  2462.5 690.1 %all-to-all-done.1 = bf16[2,16,512,1024]{3,2,0,1:T(8,128)(2,1)} async-done(((bf16[2,16,512,1024]{3,2,0,1:T(8,128)(2,1)}), bf16[2,16,512,1024]{3,2,0,1:T(8,128)(2,1)}, u32[]{:S(2)}, u32[]{:S(2)}) %all-to-all-start.1) | async-done | bytes 33554464 | tf_op jit(solution)/shard_map/all_to_all | solution.py:43
  3152.6 22.6 copy.67
  3175.2 150.6 %gather_fusion.2 = bf16[8192,1024]{1,0:T(8,128)(2,1)} fusion(bf16[16384,1024]{1,0:T(8,128)(2,1)} %bitcast.58, s32[8192]{0:T(1024)S(1)} %broadcast_clamp_fusion.1), kind=kCustom, calls=%fused_computation.2 | custom fusion | bytes 33587200 | tf_op jit(solution)/shard_map/jit(_take)/gather | solution.py:18
  3325.8 18.1 multiply_reduce_fusion
  (100 shorter events, 1.5 us)
Async XLA Ops:
  0.0 1437.4 %copy-start = (bf16[1024,1024]{1,0:T(8,128)(2,1)S(1)}, bf16[1024,1024]{1,0:T(8,128)(2,1)}, u32[]{:S(2)}) copy-start(bf16[1024,1024]{1,0:T(8,128)(2,1)} %param.8) | copy-start | bytes 6291460
  1437.2 70.0 %copy-start.2 = (s32[32,1024]{1,0:T(8,128)}, s32[32,1024]{1,0:T(8,128)S(1)}, u32[]{:S(2)}) copy-start(s32[32,1024]{1,0:T(8,128)S(1)} %get-tuple-element.149) | copy-start | bytes 393220
  2263.4 22.8 copy-start.7
  2388.2 6.4 copy-start.4
  2388.2 764.4 %all-to-all-start.1 = ((bf16[2,16,512,1024]{3,2,0,1:T(8,128)(2,1)}), bf16[2,16,512,1024]{3,2,0,1:T(8,128)(2,1)}, u32[]{:S(2)}, u32[]{:S(2)}) async-start(bf16[2,16,512,1024]{3,2,0,1:T(8,128)(2,1)} %copy.66), calls=%async_computation.1 | async-start | bytes 67108864 | tf_op jit(solution)/shard_map/all_to_all | solution.py:43
  2394.6 0.9 copy-start.3
  2395.5 66.0 %copy-start.5 = (s32[1024,8]{0,1:T(8,128)S(1)}, s32[1024,8]{0,1:T(8,128)}, u32[]{:S(2)}) copy-start(s32[1024,8]{0,1:T(8,128)} %param.9) | copy-start | bytes 98308
  2395.5 66.8 %copy-start.6 = (f32[1024,8]{0,1:T(8,128)S(1)}, f32[1024,8]{0,1:T(8,128)}, u32[]{:S(2)}) copy-start(f32[1024,8]{0,1:T(8,128)} %param.10) | copy-start | bytes 98308
  3175.2 168.7 %copy-start.1 = (bf16[1024,1024]{1,0:T(8,128)(2,1)S(1)}, bf16[1024,1024]{1,0:T(8,128)(2,1)}, u32[]{:S(2)}) copy-start(bf16[1024,1024]{1,0:T(8,128)(2,1)} %param.8) | copy-start | bytes 6291460
where the time goes:
time: 3350 us; the launch traced here: 3340 us
  local copies, waits for them, and re-layouts  1780 us (53%)
  blocking collectives  733 us (22%)
  waiting for transfers between devices  690 us (21%)
  matrix products  79.3 us (2%)
  other arithmetic  52.5 us (2%)
    gather x11, local copies, waits for them, and re-layouts, pack_index(): jnp.searchsorted(column, targets, side='left')  1420 us
    all_to_all x1, blocking collectives, local_step(): recv_buf = lax.all_to_all(send_buf, 'ep', 1, 1, tiled=True)  733 us
    all_to_all x1, waiting for transfers between devices, local_step(): lax.all_to_all(expert_out.reshape(local_n, group_n, capacity, d_model), '...  690 us
    gather x1, local copies, waits for them, and re-layouts, combine_rows(): picked = jnp.take(returned, flat_pos, axis=0)  151 us
    gather x1, local copies, waits for them, and re-layouts, local_step(): send_buf = jnp.take(tok_loc, row_ids, axis=0, mode='fill', fill_value=0)  69.7 us
  transfers between devices with their start and end apart: 1, of which 1 were waited for; matrix products, arithmetic and copies ran while one was open for 2% of the time, Pallas kernels for 0%

commit v1 on v0

v1 whole, which is shorter than its diff:
```python
import functools
import math

import jax
import jax.numpy as jnp
from jax import lax
from jax.experimental import pallas as pl
from jax.experimental.pallas import tpu as pltpu
from jax.sharding import PartitionSpec as P

CORES = 2
CHUNKS = 4
TILE = 256


def kernel(side, planes, x_ref, route_ref, gate_ref, wg_ref, wu_ref, wd_ref,
           y_ref, gs_ref, us_ref, ds_ref,
           x_all, route_all, gate_all, y_acc, y_peer, y_out, g_buf, u_buf, d_buf,
           zsend, zrecv, hsend, hrecv, load_sem, tok_sem, tok_send, tok_recv, part_send, part_recv, out_sem):
    half = planes // 2
    tok_n = x_ref.shape[0]
    rows_all = x_all.shape[0]
    tile = min(TILE, tok_n)
    tiles_half = tok_n // tile
    tiles = rows_all // tile
    col = lax.axis_index("dp")
    pos = lax.axis_index("ep")
    core = pos % CORES
    plane = pos // CORES
    cx, cy = col // side, col % side
    parity = (cx + cy) % 2
    other = 1 - parity
    col_x = col + side * (1 - 2 * (cx % 2))
    col_y = col + 1 - 2 * (cy % 2)
    up = (pos + CORES) % (planes * CORES)
    down = (pos + (planes - 1) * CORES) % (planes * CORES)
    peer = pos + 1 - 2 * core
    ring = ({"ep": up}, {"ep": down})
    side_dev = ({"dp": col_x}, {"dp": col_y})
    own = (wg_ref, wu_ref, wd_ref)
    slots = (gs_ref, us_ref, ds_ref)
    bufs = (g_buf, u_buf, d_buf)
    rows = tuple(w.shape[1] // CHUNKS for w in own)

    barrier = pltpu.get_barrier_semaphore()
    for dev in (*ring, *side_dev, {"ep": peer}):
        pl.semaphore_signal(barrier, inc=1, device_id=dev)
    pl.semaphore_wait(barrier, 5)

    def piece(which, ref, idx, i):
        return ref.at[idx, pl.ds(i * rows[which], rows[which])]

    def first_hop(way, which, i):
        return pltpu.make_async_remote_copy(
            piece(which, own[which], parity, i), piece(which, slots[which], way, i),
            zsend.at[way, 0, which, i], zrecv.at[way, 0, which, i], device_id=ring[way])

    def next_hop(way, h, which, i):
        return pltpu.make_async_remote_copy(
            piece(which, slots[which], (h - 1) * 4 + way, i), piece(which, slots[which], h * 4 + way, i),
            zsend.at[way, h, which, i], zrecv.at[way, h, which, i], device_id=ring[way])

    def side_hop(way, h, which, i):
        return pltpu.make_async_remote_copy(
            piece(which, slots[which], (h - 1) * 4 + way, i), piece(which, slots[which], (h - 1) * 4 + 2 + way, i),
            hsend.at[way, h - 1, which, i], hrecv.at[way, h - 1, which, i], device_id=side_dev[way])

    def wait_ring(way, h, which, i):
        there = piece(which, slots[which], (h - 1) * 4 + way, i)
        pltpu.make_async_remote_copy(
            there, there, zsend.at[way, h - 1, which, i], zrecv.at[way, h - 1, which, i], device_id=ring[way]).wait_recv()

    lo = half_pieces(0)
    hi = half_pieces(1)

    def halves(way):
        return lo if way == 0 else hi

    def goes_far(way, which):
        return [i for i in range(CHUNKS) if (which, i) in halves(way)]

    mine = pl.ds(core * tok_n, tok_n)
    tok = ((x_ref, x_all), (route_ref, route_all), (gate_ref, gate_all))
    for k, (src, dst) in enumerate(tok):
        pltpu.make_async_remote_copy(src, dst.at[mine], tok_send.at[k], tok_recv.at[k], device_id={"ep": peer}).start()
        pltpu.make_async_copy(src, dst.at[mine], tok_sem.at[k]).start()
    for which in range(3):
        for i in range(CHUNKS):
            for way in range(2):
                first_hop(way, which, i).start()

    def load_own(e, buf):
        for which in range(3):
            pltpu.make_async_copy(own[which].at[e], bufs[which].at[buf], load_sem.at[buf, which]).start()

    def load_slot(s, buf):
        for which in range(3):
            pltpu.make_async_copy(slots[which].at[s], bufs[which].at[buf], load_sem.at[buf, which]).start()

    def load_last(s, buf):
        for which in range(3):
            for way in range(2):
                ids = goes_far(way, which)
                if ids:
                    part = pl.ds(ids[0] * rows[which], len(ids) * rows[which])
                    pltpu.make_async_copy(slots[which].at[s + way, part], bufs[which].at[buf, part], load_sem.at[buf, which]).start()

    def wait_load(buf):
        for which in range(3):
            pltpu.make_async_copy(own[which].at[0], bufs[which].at[buf], load_sem.at[buf, which]).wait()

    def expert_id(h, q):
        src = (plane + planes + (2 * (q % 2) - 1) * h) % planes
        sub = parity + (q // 2) * (1 - 2 * parity)
        return (src * CORES + core) * 2 + sub

    def compute(row0, buf, expert):
        part = pl.ds(row0, tile)
        x_tile = x_all[part]
        a = jnp.dot(x_tile, g_buf[buf], preferred_element_type=jnp.float32)
        b = jnp.dot(x_tile, u_buf[buf], preferred_element_type=jnp.float32)
        hidden = (jax.nn.silu(a) * b).astype(jnp.bfloat16)
        out = jnp.dot(hidden, d_buf[buf], preferred_element_type=jnp.float32).astype(jnp.bfloat16)
        gate = jnp.sum(jnp.where(route_all[part] == expert, gate_all[part], 0.0), axis=1, keepdims=True)
        y_acc[part] += jnp.where(gate > 0.0, gate * out.astype(jnp.float32), 0.0)

    load_own(0, 0)
    y_acc[...] = jnp.zeros_like(y_acc)
    for k, (src, dst) in enumerate(tok):
        pltpu.make_async_copy(src, dst.at[mine], tok_sem.at[k]).wait()
        pltpu.make_async_remote_copy(src, dst.at[mine], tok_send.at[k], tok_recv.at[k], device_id={"ep": peer}).wait()

    def wait_side(way, h, ids):
        for which, i in ids:
            side_hop(way, h, which, i).wait_recv()

    every = [(which, i) for which in range(3) for i in range(CHUNKS)]

    def step_tile(h, t):
        q = t // tiles
        buf = q % 2

        @pl.when(t % tiles == 0)
        def _():
            wait_load(buf)

            @pl.when(h == 1)
            def _():
                @pl.when(q == 0)
                def _():
                    load_own(1, 1)

            @pl.when(h > 1)
            def _():
                @pl.when(q < 3)
                def _():
                    @pl.when(q == 1)
                    def _():
                        wait_side(0, h - 1, every)

                    @pl.when(q == 2)
                    def _():
                        wait_side(1, h - 1, every)

                    load_slot((h - 2) * 4 + q + 1, 1 - buf)

        first = (plane * CORES + core) * 2 + q
        expert = jnp.where(h == 1, first, expert_id(h - 1, q))
        compute((t % tiles) * tile, buf, expert)

    per_set = -(-4 * tiles // (3 * CHUNKS))

    def stage(h, carry):
        @pl.when(h > 1)
        def _():
            load_slot((h - 2) * 4, 0)

        count = jnp.where(h == 1, 2, 4) * tiles
        for which in range(3):
            def one(i, c, which=which):
                for way in range(2):
                    far = goes_far(way, which)
                    wait_ring(way, h, which, i)
                    if len(far) == CHUNKS:
                        next_hop(way, h, which, i).start()
                    else:
                        ok = h < half - 1
                        if far:
                            ok = ok | ((i >= far[0]) & (i <= far[-1]))

                        @pl.when(ok)
                        def _():
                            next_hop(way, h, which, i).start()
                    side_hop(way, h, which, i).start()

                def tile_step(k, c2):
                    t = (which * CHUNKS + i) * per_set + k

                    @pl.when(t < count)
                    def _():
                        step_tile(h, t)
                    return c2

                return lax.fori_loop(0, per_set, tile_step, c)

            lax.fori_loop(0, CHUNKS, one, 0)
        return carry

    lax.fori_loop(1, half, stage, 0)

    load_slot((half - 2) * 4, 0)
    sets = len(lo)
    per_last = -(-4 * tiles // sets)
    for k in range(sets):
        for way in range(2):
            which, i = halves(way)[k]
            wait_ring(way, half, which, i)
            side_hop(way, half, which, i).start()

        def tile_step(n, c, k=k):
            t = k * per_last + n

            @pl.when(t < 4 * tiles)
            def _():
                step_tile(half, t)
            return c

        lax.fori_loop(0, per_last, tile_step, 0)

    far_slot = (half - 1) * 4
    load_last(far_slot, 0)
    for way in range(2):
        wait_side(way, half, halves(way))
    load_last(far_slot + 2, 1)
    wait_load(0)

    def far_own(t, c):
        compute(t * tile, 0, expert_id(half, 0))
        return c

    lax.fori_loop(0, tiles, far_own, 0)
    wait_load(1)

    def part_copy(t):
        src = y_acc.at[pl.ds((1 - core) * tok_n + t * tile, tile)]
        return pltpu.make_async_remote_copy(src, y_peer.at[pl.ds(t * tile, tile)], part_send.at[t], part_recv.at[t], device_id={"ep": peer})

    def far_side(t, c):
        which_half = (1 - core) + (t // tiles_half) * (2 * core - 1)
        compute(which_half * tok_n + (t % tiles_half) * tile, 1, expert_id(half, 2))

        @pl.when((t >= 1) & (t <= tiles_half))
        def _():
            part_copy(t - 1).start()
        return c

    lax.fori_loop(0, tiles, far_side, 0)

    def finish(t, c):
        part_copy(t).wait()
        part = pl.ds(t * tile, tile)
        y_out[part] = (y_acc[pl.ds(core * tok_n + t * tile, tile)] + y_peer[part]).astype(y_out.dtype)
        pltpu.make_async_copy(y_out.at[part], y_ref.at[part], out_sem.at[t]).start()
        return c

    lax.fori_loop(0, tiles_half, finish, 0)

    def drain_out(t, c):
        part = pl.ds(t * tile, tile)
        pltpu.make_async_copy(y_out.at[part], y_ref.at[part], out_sem.at[t]).wait()
        return c

    lax.fori_loop(0, tiles_half, drain_out, 0)

    for which in range(3):
        def drain(i, c, which=which):
            for way in range(2):
                first_hop(way, which, i).wait_send()

                def per_stage(h, c2):
                    side_hop(way, h, which, i).wait_send()
                    return c2

                lax.fori_loop(1, half, per_stage, 0)

                def per_hop(h, c2):
                    next_hop(way, h, which, i).wait_send()
                    return c2

                lax.fori_loop(1, half - 1, per_hop, 0)
            return c

        lax.fori_loop(0, CHUNKS, drain, 0)
    for way in range(2):
        for which, i in halves(way):
            next_hop(way, half - 1, which, i).wait_send()
            side_hop(way, half, which, i).wait_send()


def half_pieces(way):
    mid = CHUNKS // 2
    return [(way, i) for i in range(CHUNKS)] + [(2, way * mid + i) for i in range(mid)]


def moe(side, planes, x, route, gate, wg, wu, wd):
    tok_n, d_model = x.shape
    d_ff = wg.shape[2]
    half = planes // 2
    slots = half * 4
    tile = min(TILE, tok_n)
    parts = tok_n // tile
    bf = jnp.bfloat16
    any_spec = pl.BlockSpec(memory_space=pl.ANY)
    dma = pltpu.SemaphoreType.DMA
    rows = CORES * tok_n
    out = pl.pallas_call(
        functools.partial(kernel, side, planes),
        out_shape=(
            jax.ShapeDtypeStruct((tok_n, d_model), bf),
            jax.ShapeDtypeStruct((slots, d_model, d_ff), bf),
            jax.ShapeDtypeStruct((slots, d_model, d_ff), bf),
            jax.ShapeDtypeStruct((slots, d_ff, d_model), bf),
        ),
        in_specs=[any_spec] * 6,
        out_specs=(any_spec,) * 4,
        scratch_shapes=[
            pltpu.VMEM((rows, d_model), bf),
            pltpu.VMEM((rows, route.shape[1]), jnp.int32),
            pltpu.VMEM((rows, route.shape[1]), jnp.float32),
            pltpu.VMEM((rows, d_model), jnp.float32),
            pltpu.VMEM((tok_n, d_model), jnp.float32),
            pltpu.VMEM((tok_n, d_model), bf),
            pltpu.VMEM((2, d_model, d_ff), bf),
            pltpu.VMEM((2, d_model, d_ff), bf),
            pltpu.VMEM((2, d_ff, d_model), bf),
            dma((2, half, 3, CHUNKS)),
            dma((2, half, 3, CHUNKS)),
            dma((2, half, 3, CHUNKS)),
            dma((2, half, 3, CHUNKS)),
            dma((2, 3)),
            dma((3,)),
            dma((3,)),
            dma((3,)),
            dma((parts,)),
            dma((parts,)),
            dma((parts,)),
        ],
        compiler_params=pltpu.CompilerParams(
            collective_id=0, has_side_effects=True, vmem_limit_bytes=60 * 1024 * 1024),
        name="stream_experts",
    )(x, route, gate, wg, wu, wd)
    return out[0]


def solution(mesh):
    planes = mesh.shape["ep"] // CORES
    side = math.isqrt(mesh.shape["dp"])
    row_spec = P(("dp", "ep"))
    expert_spec = P("ep")

    def local_step(tok_loc, route_loc, gate_loc, wg_loc, wu_loc, wd_loc):
        return moe(side, planes, tok_loc, route_loc, gate_loc, wg_loc, wu_loc, wd_loc)

    return jax.shard_map(local_step, mesh=mesh, in_specs=(row_spec, row_spec, row_spec, expert_spec, expert_spec, expert_spec), out_specs=row_spec, check_vma=False)
```

time: 3350 us -> 290 us (0.09)
  local copies, waits for them, and re-layouts: 1780 us -> 6.63 us
  blocking collectives: 733 us -> 0 us
  waiting for transfers between devices: 690 us -> 0 us
  Pallas kernels: 0 us -> 283 us
  matrix products: 79.3 us -> 0 us
  other arithmetic: 52.5 us -> 0 us
    gather x18 -> x0, local copies, waits for them, and re-layouts: 1710 us -> none  [the longest x11 1420 us: pack_index(): jnp.searchsorted(column, targets, side='left')]
    all_to_all x1 -> x0, blocking collectives: 733 us -> none  [local_step(): recv_buf = lax.all_to_all(send_buf, 'ep', 1, 1, tiled=True)]
    all_to_all x1 -> x0, waiting for transfers between devices: 690 us -> none  [local_step(): lax.all_to_all(expert_out.reshape(local_n, group_n, capacity, d_model), '...]
    pallas_call x0 -> x1, Pallas kernels: none -> 283 us  [moe(): pl.pallas_call(functools.partial(kernel, side, planes), out_shape=(jax.Sh...]
    dot_general x2 -> x0, matrix products: 79.3 us -> none  [the longest x1 47.6 us: expert_ffn(): jnp.einsum('erf,efd->erd', hidden, wd_loc, preferred_element_type=jnp.flo...]
    all_to_all x2 -> x0, local copies, waits for them, and re-layouts: 45.4 us -> none  [the longest x1 22.8 us: local_step(): recv_buf = lax.all_to_all(send_buf, 'ep', 1, 1, tiled=True)]
  transfers between devices with their start and end apart: 1 -> 0, of which waited for: 1 -> 0; matrix products, arithmetic and copies ran while one was open for 2% -> 0% of each run, Pallas kernels for 0% -> 0%
where the time goes in v1:
time: 290 us
  Pallas kernels  283 us (98%)
  local copies, waits for them, and re-layouts  6.63 us (2%)
    pallas_call x1, Pallas kernels, moe(): pl.pallas_call(functools.partial(kernel, side, planes), out_shape=(jax.Sh...  283 us
    unnamed x3, local copies, waits for them, and re-layouts  6.63 us

profile of v1, /device:TPU:21, one launch (start us, length us, event | category | flops | bytes accessed | tf_op | source)
XLA Modules:
  0.0 290.0 jit_solution(3218785009268141464)
XLA Ops:
  0.0 1.8 copy.7.route_ref
  1.8 1.8 copy.8.gate_ref
  3.5 283.4 %stream_experts.1 = (bf16[1024,1024]{1,0:T(8,128)(2,1)}, bf16[16,1024,512]{2,1,0:T(8,128)(2,1)}, bf16[16,1024,512]{2,1,0:T(8,128)(2,1)}, bf16[16,512,1024]{2,1,0:T(8,128)(2,1)}) custom-call(bf16[1024,1024]{1,0:T(8,128)(2,1)} %x_ref.1, s32[1024,8]{1,0:T(8,128)} %copy.7.route_ref, f32[1024,8]{1,0:T(8,128)} %copy.8.gate_ref, bf16[2,1024,512]{2,1,0:T(8,128)(2,1)} %wg_ref.1, ...), custom_call_target="tpu_custom_call" | custom-call | tf_op jit(solution)/shard_map/stream_experts/pallas_call | solution.py:316
  286.9 3.1 %copy.10 = bf16[1024,1024]{1,0:T(8,128)(2,1)} copy(bf16[1024,1024]{1,0:T(8,128)(2,1)} %get-tuple-element.6) | data formatting | bytes 4194304

commit v2 on v0

v2 whole, which is shorter than its diff:
```python
import functools
import math

import jax
import jax.numpy as jnp
from jax import lax
from jax.experimental import pallas as pl
from jax.experimental.pallas import tpu as pltpu
from jax.sharding import PartitionSpec as P

CORES = 2
CHUNKS = 8
TILE = 256
LANES = 128


def kernel(side, planes, x_ref, route_ref, gate_ref, wg_ref, wu_ref, wd_ref,
           y_ref, gs_ref, us_ref, ds_ref,
           x_all, route_all, gate_all, gate_rows, gate_cols, y_acc, y_peer, hidden,
           g_buf, u_buf, d_buf, g_far, u_far, d_far,
           zsend, zrecv, hsend, hrecv, psend, precv, gu_sem, d_sem, tok_sem, tok_send, tok_recv, part_send, part_recv):
    half = planes // 2
    tok_n = x_ref.shape[0]
    tile = min(TILE, tok_n)
    tiles_half = tok_n // tile
    tiles = CORES * tiles_half
    experts = planes * CORES * 2
    col = lax.axis_index("dp")
    pos = lax.axis_index("ep")
    core = pos % CORES
    plane = pos // CORES
    cx, cy = col // side, col % side
    parity = (cx + cy) % 2
    col_x = col + side * (1 - 2 * (cx % 2))
    col_y = col + 1 - 2 * (cy % 2)
    up = (pos + CORES) % (planes * CORES)
    down = (pos + (planes - 1) * CORES) % (planes * CORES)
    peer = {"ep": pos + 1 - 2 * core}
    ring = ({"ep": up}, {"ep": down})
    side_dev = ({"dp": col_x}, {"dp": col_y})
    own = (wg_ref, wu_ref, wd_ref)
    slots = (gs_ref, us_ref, ds_ref)
    far = (g_far, u_far, d_far)
    rows = tuple(w.shape[1] // CHUNKS for w in own)
    mid = CHUNKS // 2
    mine = core * tok_n
    theirs = (1 - core) * tok_n
    remote = pltpu.make_async_remote_copy

    barrier = pltpu.get_barrier_semaphore()
    for dev in (*ring, *side_dev, peer):
        pl.semaphore_signal(barrier, inc=1, device_id=dev)
    pl.semaphore_wait(barrier, 5)

    def piece(which, ref, idx, i):
        return ref.at[idx, pl.ds(i * rows[which], rows[which])]

    def first_hop(way, which, i):
        return remote(piece(which, own[which], parity, i), piece(which, slots[which], way, i),
                      zsend.at[way, 0, which, i], zrecv.at[way, 0, which, i], device_id=ring[way])

    def next_hop(way, h, which, i):
        return remote(piece(which, slots[which], (h - 1) * 4 + way, i), piece(which, slots[which], h * 4 + way, i),
                      zsend.at[way, h, which, i], zrecv.at[way, h, which, i], device_id=ring[way])

    def last_hop(way, which, i):
        return remote(piece(which, slots[which], (half - 2) * 4 + way, i), piece(which, far[which], 0, i),
                      zsend.at[way, half - 1, which, i], zrecv.at[way, half - 1, which, i], device_id=ring[way])

    def side_hop(way, h, which, i):
        return remote(piece(which, slots[which], (h - 1) * 4 + way, i), piece(which, slots[which], (h - 1) * 4 + 2 + way, i),
                      hsend.at[way, h - 1, which, i], hrecv.at[way, h - 1, which, i], device_id=side_dev[way])

    def far_side(way, which, i):
        return remote(piece(which, far[which], 0, i), piece(which, far[which], 2, i),
                      hsend.at[way, half - 1, which, i], hrecv.at[way, half - 1, which, i], device_id=side_dev[way])

    def to_peer(kind, which, i):
        return remote(piece(which, far[which], 2 * kind, i), piece(which, far[which], 2 * kind + 1, i),
                      psend.at[kind, which, i], precv.at[kind, which, i], device_id=peer)

    def wait_ring(way, h, which, i):
        there = piece(which, slots[which], (h - 1) * 4 + way, i)
        remote(there, there, zsend.at[way, h - 1, which, i], zrecv.at[way, h - 1, which, i], device_id=ring[way]).wait_recv()

    def wait_side(h, which):
        def one(i, c):
            for way in range(2):
                side_hop(way, h, which, i).wait_recv()
            return c

        lax.fori_loop(0, CHUNKS, one, 0)

    for which in range(3):
        def start(i, c, which=which):
            for way in range(2):
                first_hop(way, which, i).start()
            return c

        lax.fori_loop(0, CHUNKS, start, 0)

    def load_gu(refs, idx, b):
        for m, buf in enumerate((g_buf, u_buf)):
            pltpu.make_async_copy(refs[m].at[idx], buf.at[b], gu_sem.at[b, m]).start()

    def wait_gu(b):
        for m, buf in enumerate((g_buf, u_buf)):
            pltpu.make_async_copy(own[m].at[0], buf.at[b], gu_sem.at[b, m]).wait()

    def load_d(ref, idx, b):
        pltpu.make_async_copy(ref.at[idx], d_buf.at[b], d_sem.at[b]).start()

    def wait_d(b):
        pltpu.make_async_copy(wd_ref.at[0], d_buf.at[b], d_sem.at[b]).wait()

    load_gu(own, 0, 0)
    load_gu(own, 1, 1)
    my_rows = pl.ds(mine, tok_n)
    tok = ((x_ref, x_all.at[my_rows]), (route_ref, route_all.at[core]), (gate_ref, gate_all.at[core]))
    for k, (src, dst) in enumerate(tok):
        remote(src, dst, tok_send.at[k], tok_recv.at[k], device_id=peer).start()
        pltpu.make_async_copy(src, dst, tok_sem.at[k]).start()
    y_acc[...] = jnp.zeros_like(y_acc)
    gate_rows[...] = jnp.zeros_like(gate_rows)
    for k, (src, dst) in reversed(list(enumerate(tok))):
        pltpu.make_async_copy(src, dst, tok_sem.at[k]).wait()
        remote(src, dst, tok_send.at[k], tok_recv.at[k], device_id=peer).wait()

    def dense(c, carry):
        route, gate = route_all[c], gate_all[c]
        for e in range(experts):
            gate_rows[e:e + 1, :] = jnp.sum(jnp.where(route == e, gate, 0.0), axis=0, keepdims=True)
        for b in range(tok_n // LANES):
            gate_cols[pl.ds(c * tok_n + b * LANES, LANES), :] = gate_rows[:, b * LANES:(b + 1) * LANES].T
        return carry

    lax.fori_loop(0, CORES, dense, 0)

    def expert_id(h, q, ring_core):
        src = (plane + planes + (2 * (q % 2) - 1) * h) % planes
        sub = parity + (q // 2) * (1 - 2 * parity)
        return (src * CORES + ring_core) * 2 + sub

    def front(row0, g, u, q, out0):
        x_tile = x_all[pl.ds(row0, tile)]
        a = jnp.dot(x_tile, g, preferred_element_type=jnp.float32)
        b = jnp.dot(x_tile, u, preferred_element_type=jnp.float32)
        hidden[q, pl.ds(out0, tile)] = (jax.nn.silu(a) * b).astype(jnp.bfloat16)

    def back(q, h0, d, row0, expert):
        out = jnp.dot(hidden[q, pl.ds(h0, tile)], d, preferred_element_type=jnp.float32).astype(jnp.bfloat16)
        gates = gate_cols[pl.ds(row0, tile)]
        lane = lax.broadcasted_iota(jnp.int32, gates.shape, 1)
        gate = jnp.sum(jnp.where(lane == expert, gates, 0.0), axis=1, keepdims=True)
        return jnp.where(gate > 0.0, gate * out.astype(jnp.float32), 0.0)

    def front_tile(t, q0):
        e, r = t // tiles, t % tiles

        @pl.when(r == 0)
        def _():
            wait_gu(e)

        front(r * tile, g_buf[e], u_buf[e], q0 + e, r * tile)

    def back_tile(t, stage):
        q, r = t // tiles, t % tiles

        @pl.when(r == 0)
        def _():
            wait_d(q)

        expert = jnp.where(stage == 0, (plane * CORES + core) * 2 + q, expert_id(stage, q, core))
        y_acc[pl.ds(r * tile, tile)] += back(q, r * tile, d_buf[q], r * tile, expert)

    def run(tile_fn, first, count, arg):
        def one(k, c):
            tile_fn(first + k, arg)
            return c

        lax.fori_loop(0, count, one, 0)

    def late_pair(h):
        for which in range(2):
            wait_side(h, which)
        load_gu(slots, (h - 1) * 4 + 2, 0)
        load_gu(slots, (h - 1) * 4 + 3, 1)

    def downs(h):
        wait_side(h, 2)
        for q in range(4):
            load_d(ds_ref, (h - 1) * 4 + q, q)

    per_front = 2 * tiles // CHUNKS
    per_back = 4 * tiles // CHUNKS
    halves = ([(0, i) for i in range(CHUNKS)] + [(2, i) for i in range(mid)],
              [(1, i) for i in range(CHUNKS)] + [(2, mid + i) for i in range(mid)])

    def stage(h, carry):
        for which in range(3):
            if which == 0:
                @pl.when(h > 1)
                def _():
                    late_pair(h - 1)
            elif which == 1:
                @pl.when(h == 1)
                def _():
                    load_d(wd_ref, 0, 0)
                    load_d(wd_ref, 1, 1)

                @pl.when(h > 1)
                def _():
                    downs(h - 1)
            else:
                load_gu(slots, (h - 1) * 4, 0)
                load_gu(slots, (h - 1) * 4 + 1, 1)

            def one(i, c, which=which):
                for way in range(2):
                    wait_ring(way, h, which, i)
                    far_ids = [k for w, k in halves[way] if w == which]

                    @pl.when(h < half - 1)
                    def _():
                        next_hop(way, h, which, i).start()

                    if far_ids:
                        @pl.when((h == half - 1) & (i >= far_ids[0]) & (i <= far_ids[-1]))
                        def _():
                            last_hop(way, which, i).start()
                    side_hop(way, h, which, i).start()
                if which == 0:
                    run(front_tile, i * per_front, per_front, 2 - 2 * jnp.where(h == 1, 1, 0))
                elif which == 1:
                    n = jnp.where(h == 1, per_back // 2, per_back)
                    run(back_tile, i * n, n, h - 1)
                else:
                    run(front_tile, i * per_front, per_front, 0)
                return c

            lax.fori_loop(0, CHUNKS, one, 0)
        return carry

    lax.fori_loop(1, half, stage, 0)

    def far_ring(way, which, i):
        last_hop(way, which, i).wait_recv()
        far_side(way, which, i).start()
        to_peer(0, which, i).start()

    def far_cross(way, which, i):
        far_side(way, which, i).wait_recv()
        to_peer(1, which, i).start()

    late_pair(half - 1)

    def far_a(i, c):
        for way in range(2):
            far_ring(way, way, i)

        @pl.when(i >= 2)
        def _():
            for way in range(2):
                far_cross(way, way, i - 2)
        run(front_tile, i * 2 * per_front, 2 * per_front, 2)
        return c

    lax.fori_loop(0, mid, far_a, 0)
    downs(half - 1)

    def far_b(i, c):
        for way in range(2):
            far_ring(way, way, i)
            far_cross(way, way, i - 2)
        run(back_tile, (i - mid) * 2 * per_back, 2 * per_back, half - 1)
        return c

    lax.fori_loop(mid, CHUNKS, far_b, 0)

    def part_copy(t):
        src = y_acc.at[pl.ds(theirs + t * tile, tile)]
        return remote(src, y_peer.at[pl.ds(t * tile, tile)], part_send.at[t], part_recv.at[t], device_id=peer)

    def far_front(f):
        def one(t, c):
            front(mine + t * tile, g_far[f], u_far[f], f, t * tile)
            return c

        lax.fori_loop(0, tiles_half, one, 0)

    def wait_peer(kind, which):
        def one(i, c):
            to_peer(kind, which, i).wait_recv()
            return c

        lax.fori_loop(0, CHUNKS, one, 0)

    for n in range(mid):
        for way in range(2):
            far_ring(way, 2, way * mid + n)
            if n < 2:
                far_cross(way, way, CHUNKS - 2 + n)
            else:
                far_cross(way, 2, way * mid + n - 2)
        if n == 1:
            for t in range(tiles_half):
                part_copy(t).start()
        if n % 2 == 1:
            for which in range(2):
                wait_peer(n // 2, which)
        if n < 4:
            far_front(n)

    def far_back(f, expert):
        def one(t, c):
            y_acc[pl.ds(mine + t * tile, tile)] += back(f, t * tile, d_far[f], mine + t * tile, expert)
            return c

        lax.fori_loop(0, tiles_half, one, 0)

    far_back(0, expert_id(half, 0, core))
    for way in range(2):
        far_cross(way, 2, way * mid + mid - 2)
    wait_peer(0, 2)
    far_back(1, expert_id(half, 0, 1 - core))
    for way in range(2):
        far_cross(way, 2, way * mid + mid - 1)
    far_back(2, expert_id(half, 2, core))
    for t in range(tiles_half):
        part_copy(t).wait()
    wait_peer(1, 2)

    def finish(t, c):
        part = pl.ds(t * tile, tile)
        row0 = mine + t * tile
        total = y_acc[pl.ds(row0, tile)] + y_peer[part] + back(3, t * tile, d_far[3], row0, expert_id(half, 2, 1 - core))
        y_ref[part] = total.astype(y_ref.dtype)
        return c

    lax.fori_loop(0, tiles_half, finish, 0)

    for which in range(3):
        def drain(i, c, which=which):
            for way in range(2):
                first_hop(way, which, i).wait_send()

                def per_stage(h, c2):
                    side_hop(way, h, which, i).wait_send()
                    return c2

                lax.fori_loop(1, half, per_stage, 0)

                def per_hop(h, c2):
                    next_hop(way, h, which, i).wait_send()
                    return c2

                lax.fori_loop(1, half - 1, per_hop, 0)
            for kind in range(2):
                to_peer(kind, which, i).wait_send()
            return c

        lax.fori_loop(0, CHUNKS, drain, 0)
    for way in range(2):
        for which, i in halves[way]:
            last_hop(way, which, i).wait_send()
            far_side(way, which, i).wait_send()


def moe(side, planes, x, route, gate, wg, wu, wd):
    tok_n, d_model = x.shape
    d_ff = wg.shape[2]
    half = planes // 2
    slots = (half - 1) * 4
    parts = tok_n // min(TILE, tok_n)
    bf = jnp.bfloat16
    f32 = jnp.float32
    any_spec = pl.BlockSpec(memory_space=pl.ANY)
    dma = pltpu.SemaphoreType.DMA
    rows = CORES * tok_n
    top_k = route.shape[0]
    out = pl.pallas_call(
        functools.partial(kernel, side, planes),
        out_shape=(
            jax.ShapeDtypeStruct((tok_n, d_model), bf),
            jax.ShapeDtypeStruct((slots, d_model, d_ff), bf),
            jax.ShapeDtypeStruct((slots, d_model, d_ff), bf),
            jax.ShapeDtypeStruct((slots, d_ff, d_model), bf),
        ),
        in_specs=[any_spec] * 6,
        out_specs=(pl.BlockSpec(memory_space=pltpu.VMEM),) + (any_spec,) * 3,
        scratch_shapes=[
            pltpu.VMEM((rows, d_model), bf),
            pltpu.VMEM((CORES, top_k, tok_n), jnp.int32),
            pltpu.VMEM((CORES, top_k, tok_n), f32),
            pltpu.VMEM((LANES, tok_n), f32),
            pltpu.VMEM((rows, LANES), f32),
            pltpu.VMEM((rows, d_model), f32),
            pltpu.VMEM((tok_n, d_model), f32),
            pltpu.VMEM((4, rows, d_ff), bf),
            pltpu.VMEM((2, d_model, d_ff), bf),
            pltpu.VMEM((2, d_model, d_ff), bf),
            pltpu.VMEM((4, d_ff, d_model), bf),
            pltpu.VMEM((4, d_model, d_ff), bf),
            pltpu.VMEM((4, d_model, d_ff), bf),
            pltpu.VMEM((4, d_ff, d_model), bf),
            dma((2, half, 3, CHUNKS)),
            dma((2, half, 3, CHUNKS)),
            dma((2, half, 3, CHUNKS)),
            dma((2, half, 3, CHUNKS)),
            dma((2, 3, CHUNKS)),
            dma((2, 3, CHUNKS)),
            dma((2, 2)),
            dma((4,)),
            dma((3,)),
            dma((3,)),
            dma((3,)),
            dma((parts,)),
            dma((parts,)),
        ],
        compiler_params=pltpu.CompilerParams(
            collective_id=0, has_side_effects=True, vmem_limit_bytes=50 * 1024 * 1024),
        name="stream_experts",
    )(x, route, gate, wg, wu, wd)
    return out[0]


def solution(mesh):
    planes = mesh.shape["ep"] // CORES
    side = math.isqrt(mesh.shape["dp"])
    row_spec = P(("dp", "ep"))
    expert_spec = P("ep")

    def local_step(tok_loc, route_loc, gate_loc, wg_loc, wu_loc, wd_loc):
        return moe(side, planes, tok_loc, route_loc.T, gate_loc.T, wg_loc, wu_loc, wd_loc)

    return jax.shard_map(local_step, mesh=mesh, in_specs=(row_spec, row_spec, row_spec, expert_spec, expert_spec, expert_spec), out_specs=row_spec, check_vma=False)
```

time: 3350 us -> 278 us (0.08)
  local copies, waits for them, and re-layouts: 1780 us -> 2.84 us
  blocking collectives: 733 us -> 0 us
  waiting for transfers between devices: 690 us -> 0 us
  Pallas kernels: 0 us -> 275 us
  matrix products: 79.3 us -> 0 us
  other arithmetic: 52.5 us -> 0 us
    gather x18 -> x0, local copies, waits for them, and re-layouts: 1710 us -> none  [the longest x11 1420 us: pack_index(): jnp.searchsorted(column, targets, side='left')]
    all_to_all x1 -> x0, blocking collectives: 733 us -> none  [local_step(): recv_buf = lax.all_to_all(send_buf, 'ep', 1, 1, tiled=True)]
    all_to_all x1 -> x0, waiting for transfers between devices: 690 us -> none  [local_step(): lax.all_to_all(expert_out.reshape(local_n, group_n, capacity, d_model), '...]
    pallas_call x0 -> x1, Pallas kernels: none -> 275 us  [moe(): pl.pallas_call(functools.partial(kernel, side, planes), out_shape=(jax.Sh...]
    dot_general x2 -> x0, matrix products: 79.3 us -> none  [the longest x1 47.6 us: expert_ffn(): jnp.einsum('erf,efd->erd', hidden, wd_loc, preferred_element_type=jnp.flo...]
    all_to_all x2 -> x0, local copies, waits for them, and re-layouts: 45.4 us -> none  [the longest x1 22.8 us: local_step(): recv_buf = lax.all_to_all(send_buf, 'ep', 1, 1, tiled=True)]
  transfers between devices with their start and end apart: 1 -> 0, of which waited for: 1 -> 0; matrix products, arithmetic and copies ran while one was open for 2% -> 0% of each run, Pallas kernels for 0% -> 0%
where the time goes in v2:
time: 278 us
  Pallas kernels  275 us (99%)
  local copies, waits for them, and re-layouts  2.84 us (1%)
    pallas_call x1, Pallas kernels, moe(): pl.pallas_call(functools.partial(kernel, side, planes), out_shape=(jax.Sh...  275 us

profile of v2, /device:TPU:21, one launch (start us, length us, event | category | flops | bytes accessed | tf_op | source)
XLA Modules:
  0.0 278.0 jit_solution(560447219205913613)
XLA Ops:
  0.0 0.0 copy-start
  0.0 0.8 copy-done
  0.8 0.0 copy-start.1
  0.8 0.8 copy-done.1
  1.5 275.1 %stream_experts.1 = (bf16[1024,1024]{1,0:T(8,128)(2,1)S(1)}, bf16[12,1024,512]{2,1,0:T(8,128)(2,1)}, bf16[12,1024,512]{2,1,0:T(8,128)(2,1)}, bf16[12,512,1024]{2,1,0:T(8,128)(2,1)}) custom-call(bf16[1024,1024]{1,0:T(8,128)(2,1)} %x_ref.1, s32[8,1024]{1,0:T(8,128)S(1)} %bitcast.2, f32[8,1024]{1,0:T(8,128)S(1)} %bitcast.3, bf16[2,1024,512]{2,1,0:T(8,128)(2,1)} %wg_ref.1, ...), custom_call_target="tpu_custom_call" | custom-call | tf_op jit(solution)/shard_map/stream_experts/pallas_call | solution.py:381
  276.6 1.3 copy.8
Async XLA Ops:
  0.0 0.8 copy-start
  0.8 0.8 copy-start.1

commit v3 on v2

--- a/solution.py
+++ b/solution.py
@@ -9,7 +9,7 @@
 from jax.sharding import PartitionSpec as P
 
 CORES = 2
-CHUNKS = 8
+CHUNKS = 4
 TILE = 256
 LANES = 128
 
@@ -302,14 +302,14 @@
                 far_cross(way, way, CHUNKS - 2 + n)
             else:
                 far_cross(way, 2, way * mid + n - 2)
-        if n == 1:
+        if n == mid // 2:
             for t in range(tiles_half):
                 part_copy(t).start()
-        if n % 2 == 1:
-            for which in range(2):
-                wait_peer(n // 2, which)
-        if n < 4:
-            far_front(n)
+        for f in range(n * 4 // mid, (n + 1) * 4 // mid):
+            if f % 2 == 1:
+                for which in range(2):
+                    wait_peer(f // 2, which)
+            far_front(f)
 
     def far_back(f, expert):
         def one(t, c):
@@ -386,7 +386,7 @@
             jax.ShapeDtypeStruct((slots, d_model, d_ff), bf),
             jax.ShapeDtypeStruct((slots, d_ff, d_model), bf),
         ),
-        in_specs=[any_spec] * 6,
+        in_specs=[pl.BlockSpec(memory_space=pltpu.HBM)] * 6,
         out_specs=(pl.BlockSpec(memory_space=pltpu.VMEM),) + (any_spec,) * 3,
         scratch_shapes=[
             pltpu.VMEM((rows, d_model), bf),

time: 278 us -> 275 us (0.989)
  Pallas kernels: 275 us -> 272 us
    pallas_call x1, Pallas kernels: 275 us -> 272 us  [moe(): pl.pallas_call(functools.partial(kernel, side, planes), out_shape=(jax.Sh...]
where the time goes in v3:
time: 275 us
  Pallas kernels  272 us (99%)
  local copies, waits for them, and re-layouts  2.84 us (1%)
    pallas_call x1, Pallas kernels, moe(): pl.pallas_call(functools.partial(kernel, side, planes), out_shape=(jax.Sh...  272 us

profile of v3, /device:TPU:21, one launch (start us, length us, event | category | flops | bytes accessed | tf_op | source)
XLA Modules:
  0.0 274.9 jit_solution(16697580221734957108)
XLA Ops:
  0.0 0.0 copy-start
  0.0 0.8 copy-done
  0.8 0.0 copy-start.1
  0.8 0.8 copy-done.1
  1.5 272.0 %stream_experts.1 = (bf16[1024,1024]{1,0:T(8,128)(2,1)S(1)}, bf16[12,1024,512]{2,1,0:T(8,128)(2,1)}, bf16[12,1024,512]{2,1,0:T(8,128)(2,1)}, bf16[12,512,1024]{2,1,0:T(8,128)(2,1)}) custom-call(bf16[1024,1024]{1,0:T(8,128)(2,1)} %x_ref.1, s32[8,1024]{1,0:T(8,128)S(1)} %bitcast.2, f32[8,1024]{1,0:T(8,128)S(1)} %bitcast.3, bf16[2,1024,512]{2,1,0:T(8,128)(2,1)} %wg_ref.1, ...), custom_call_target="tpu_custom_call" | custom-call | tf_op jit(solution)/shard_map/stream_experts/pallas_call | solution.py:381
  273.6 1.3 copy.8
Async XLA Ops:
  0.0 0.8 copy-start
  0.8 0.8 copy-start.1
